TPU v7x, 32 devices: a whole 2x2x4 slice. The times are simulated.
32 devices in a mesh: row: 4 (over y, core), col: 8 (over z, x).
Axes of the slice: x: 2, y: 2, z: 4, core: 2. Of those that a mesh axis runs over, the one named last changes fastest.
Arguments:
- offsets: float32 [3, 8192], P(None, ('row', 'col')), may hold values from 0 to 11
- cells: int32 [3, 64], replicated, may hold values from 0 to 3, as said below
- types: int32 [8192], P(('row', 'col')), may hold values from 0 to 3, as said below
- mask: int32 [4, 16, 4, 16], P(None, 'col', 'row'), may hold values from 0 to 1, as said below
- chi_table: float32 [4], replicated, may hold values from 2 to 10.1
- eta_table: float32 [4], replicated, may hold values from 13 to 18
- gamma_table: float32 [4], replicated, may hold values from 0.4 to 0.8
Outputs:
- charges: float32 [8192], P(('row', 'col'))
Inputs may be any that keep to these rules, and one draw needn't show every extreme that they name: The cells of the blocks are a permutation of all 4 x 4 x 4 cells: each cell holds exactly one block. The mask marks a pair of blocks exactly when their cells are equal or adjacent on the periodic grid in every dimension; it is symmetric and each block is marked with exactly 27 blocks, itself included. `types`: types 2 and 3 grow more common along the atoms, from none in the first 256 atoms to nearly all in the last.
All inputs are finite; a program needn't handle non-finite values.
Results may differ from a plain program's by a relative error of at most 0.0003.
Values sent between devices are 32-bit elements; how exact they have to be, the bound alone decides.
No kernel may reach another device: no remote copies, remote signals or barrier semaphores. Data moves between devices by JAX's collectives and lax.ppermute only.
A program may use at most 64 MiB of HBM per device.

v0:
```python
import jax
import jax.numpy as jnp
from jax import lax
from jax.sharding import PartitionSpec as P

BLOCK = 128
GRID_Z = 4
ITERS = 3
coulomb = 14.4
cutoff = 10.0
cell_side = 11.0
pair_group = 64


def taper(dist):
    xval = dist / cutoff
    poly = 1.0 + xval**4 * (-35.0 + xval * (84.0 + xval * (-70.0 + 20.0 * xval)))
    return jnp.where(xval < 1.0, poly, 0.0)


def coupling(tgt, src, tgt_cell, src_cell, same, grid):
    half = grid[:, None] // 2
    shift = ((src_cell - tgt_cell + half) % grid[:, None] - half).astype(jnp.float32) * cell_side
    radius_sq = jnp.zeros((tgt.shape[1], tgt.shape[2], src.shape[2]), jnp.float32)
    for comp in range(3):
        delta = shift[comp][:, None, None] + src[comp][:, None, :] - tgt[comp][:, :, None]
        radius_sq = radius_sq + delta * delta
    dist = jnp.sqrt(radius_sq)
    paired = tgt[3][:, :, None] * src[3][:, None, :]
    shield = 1.0 / (paired * jnp.sqrt(paired))
    kern = coulomb * taper(dist) / jnp.cbrt(radius_sq * dist + shield)
    width = tgt.shape[2]
    diag = jnp.arange(width)[:, None] == jnp.arange(width)[None, :]
    return jnp.where(same[:, None, None] & diag[None], 0.0, kern)


def pick(kinds, table):
    return jnp.sum(jnp.where(kinds, table[:, None], 0.0), axis=0)


def paired_sums(residual, image):
    return lax.psum(
        (jnp.sum(residual * residual, axis=1), jnp.sum(residual * image, axis=1)), ("row", "col")
    )


def per_device(offsets, cells, types, mask, chi_table, eta_table, gamma_table):
    n_row = lax.axis_size("row")
    n_col = lax.axis_size("col")
    row_at = lax.axis_index("row")
    col_at = lax.axis_index("col")
    span = types.shape[0]
    bpd = span // BLOCK
    n_tgt = n_row * bpd
    n_src = n_col * bpd
    grid = jnp.array([n_row, n_src // GRID_Z, GRID_Z], jnp.int32)
    kinds = jnp.arange(chi_table.shape[0])[:, None] == types[None, :]
    chi = pick(kinds, chi_table)
    eta = pick(kinds, eta_table)
    gamma = pick(kinds, gamma_table)
    geo = jnp.concatenate([offsets, gamma[None]], axis=0)
    src_geo = lax.all_gather(geo, "col", axis=1, tiled=True).reshape(4, n_src, BLOCK)
    tgt_geo = lax.all_gather(geo, "row", axis=1, tiled=True).reshape(4, n_tgt, BLOCK)
    tgt_ids = (
        (jnp.arange(n_row, dtype=jnp.int32)[:, None] * n_col + col_at) * bpd
        + jnp.arange(bpd, dtype=jnp.int32)[None, :]
    ).reshape(n_tgt)
    src_ids = row_at * n_src + jnp.arange(n_src, dtype=jnp.int32)
    tgt_cells = jnp.take(cells, tgt_ids, axis=1)
    src_cells = jnp.take(cells, src_ids, axis=1)
    tile = mask.reshape(n_tgt * n_src)
    count = jnp.sum(tile)
    slots = jnp.nonzero(tile, size=n_tgt * n_src + pair_group, fill_value=0)[0].astype(jnp.int32)
    groups = (count + pair_group - 1) // pair_group
    tgt_range = jnp.arange(n_tgt, dtype=jnp.int32)

    def block_kernel(step):
        picked = lax.dynamic_slice_in_dim(slots, step * pair_group, pair_group)
        live = step * pair_group + jnp.arange(pair_group) < count
        tgt_blk = picked // n_src
        src_blk = picked % n_src
        kern = coupling(
            tgt_geo[:, tgt_blk],
            src_geo[:, src_blk],
            tgt_cells[:, tgt_blk],
            src_cells[:, src_blk],
            tgt_ids[tgt_blk] == src_ids[src_blk],
            grid,
        )
        return (jnp.where(live[:, None, None], kern, 0.0), tgt_blk, src_blk)

    def apply(direction):
        remote = lax.all_gather(direction, "col", axis=1, tiled=True).reshape(2, n_src, BLOCK)

        def turn(step, acc):
            kern, tgt_blk, src_blk = block_kernel(step)
            contrib = jnp.einsum(
                "gij,kgj->kgi", kern, remote[:, src_blk], precision=lax.Precision.HIGHEST
            )
            owners = (tgt_range[:, None] == tgt_blk[None, :]).astype(jnp.float32)
            return acc + jnp.einsum("tg,kgi->kti", owners, contrib, precision=lax.Precision.HIGHEST)

        acc = lax.fori_loop(0, groups, turn, jnp.zeros((2, n_tgt, BLOCK), jnp.float32))
        summed = lax.psum_scatter(
            acc.reshape(2, n_tgt * BLOCK), "row", scatter_dimension=1, tiled=True
        )
        return summed + eta[None] * direction

    rhs = jnp.stack([-chi, -jnp.ones_like(chi)], axis=0)
    solution = jnp.zeros_like(rhs)
    residual = rhs
    image = apply(residual)
    norm_now, product = paired_sums(residual, image)
    alpha = norm_now / product
    direction = residual
    along = image
    for step in range(ITERS):
        solution = solution + alpha[:, None] * direction
        residual = residual - alpha[:, None] * along
        if step + 1 < ITERS:
            image = apply(residual)
            norm_next, product = paired_sums(residual, image)
            ratio = norm_next / norm_now
            alpha = norm_next / (product - ratio * norm_next / alpha)
            direction = residual + ratio[:, None] * direction
            along = image + ratio[:, None] * along
            norm_now = norm_next
    totals = lax.psum(jnp.sum(solution, axis=1), ("row", "col"))
    return solution[0] - totals[0] / totals[1] * solution[1]


def solution(mesh):
    placed = (
        P(None, ("row", "col")),
        P(),
        P(("row", "col")),
        P(None, "col", "row", None),
        P(),
        P(),
        P(),
    )
    return jax.shard_map(
        per_device, mesh=mesh, in_specs=placed, out_specs=P(("row", "col")), check_vma=False
    )
```

profile of v0, /device:TPU:0, one launch (start us, length us, event | category | flops | bytes accessed | tf_op | source)
XLA Modules:
  0.0 517.9 jit_solution(5208578501713423526)
XLA Ops:
  6.5 1.4 fusion.200
  10.3 32.4 %all_gather.16 = f32[4,2048]{1,0:T(4,128)S(1)} all-gather(f32[4,256]{1,0:T(4,128)S(1)} %pad_maximum_fusion), channel_id=1, replica_groups=mesh['row'=4,'col'=8] {'col'}, dimensions={1}, use_global_device_ids=true | all-gather | bytes 36864 | tf_op jit(solution)/shard_map/all_gather | solution.py:62
  42.7 5.2 %all_gather.17 = f32[4,1024]{1,0:T(4,128)S(1)} all-gather(f32[4,256]{1,0:T(4,128)S(1)} %pad_maximum_fusion), channel_id=1, replica_groups=mesh['row'=4,'col'=8] {'row'}, dimensions={1}, use_global_device_ids=true | all-gather | bytes 20480 | tf_op jit(solution)/shard_map/all_gather | solution.py:63
  49.1 1.4 scatter_custom_fusion
  52.3 26.1 %all_gather.15 = f32[2,2048]{1,0:T(2,128)S(1)} all-gather(f32[2,256]{1,0:T(2,128)S(1)} %stack.2), channel_id=1, replica_groups=mesh['row'=4,'col'=8] {'col'}, dimensions={1}, use_global_device_ids=true | all-gather | bytes 18432 | tf_op jit(solution)/shard_map/all_gather | solution.py:93
  79.2 28.1 %while.48 = (s32[]{:T(128)}, f32[2,8,128]{2,1,0:T(8,128)S(1)}, s32[]{:T(128)}, s32[192]{0:T(256)S(1)}, f32[2,16,128]{2,0,1:T(2,128)S(1)}, /*index=5*/s32[]{:T(12...) while((s32[]{:T(128)}, f32[2,8,128]{2,1,0:T(8,128)S(1)}, ...), condition=%wide.region_11.13_spmd.clone.clone.clone, body=%wide.region_10.12_spmd.sunk.clone.clone.clone.sunk | while | flops 59296340 | bytes 1905783 | solution.py:103
  80.8 5.6 %fusion.258 = (pred[64]{0:T(512)(128)(4,1)S(1)}, s32[64]{0:T(128)S(1)}, pred[64]{0:T(512)(128)(4,1)S(1)}) fusion(s32[64]{0:T(128)S(1)} %gather_fusion.1, s32[]{:T(128)} %bitcast.211, s32[]{:T(128)} %bitcast.212, s32[]{:T(128)} %bitcast.213, s32[]{:T(128)} %bitcast.214, s32[]{:T(128)} %bitcast.215, s32[]{:T(128)} %bitcast.216, s32[]{:T(128)} %bitcast.217, ...), kind=kLoop, calls=%fused_computation.109.clone.1 | loop fusion | flops 2048 | bytes 1196 | tf_op jit(solution)/shard_map/while/body/eq | solution.py:87
  90.3 16.9 %fusion.261 = f32[2,64,128]{2,0,1:T(2,128)S(1)} fusion(f32[64,128]{1,0:T(8,128)S(1)} %bitcast.296, f32[64,128]{1,0:T(8,128)S(1)} %bitcast.302, f32[64,128]{1,0:T(8,128)S(1)} %bitcast.300, f32[64,128]{1,0:T(8,128)S(1)} %broadcast_add_fusion.18, f32[64,128]{1,0:T(8,128)S(1)} %bitcast.301, f32[64,128]{1,0:T(8,128)S(1)} %broadcast_add_fusion.19, ...), kind=kOutput, calls=%fused_computation.71.clone.1 | convolution fusion | flops 57671680 | bytes 409728 | tf_op jit(solution)/shard_map/while/body/gij,kgj->kgi/dot_general | solution.py:97
  108.5 42.6 %reduce-scatter.10.cloned.1.call-done = f32[256,2]{1,0:T(8,128)} async-done(((f32[1024,2]{1,0:T(8,128)}), f32[256,2]{1,0:T(8,128)}) %reduce-scatter.10.cloned.1.call-update) | async-done | bytes 2064
  152.2 39.3 %all-reduce.4 = (f32[2]{0:T(128)S(1)}, f32[2]{0:T(128)S(1)}) all-reduce(f32[2]{0:T(128)S(1)} %get-tuple-element.1154, f32[2]{0:T(128)S(1)} %get-tuple-element.1153), channel_id=1, replica_groups=mesh['row'=4,'col'=8] {'row','col'}, use_global_device_ids=true, to_apply=%region_2.3 | all-reduce | flops 4 | bytes 32 | tf_op jit(solution)/shard_map/psum | solution.py:42
  191.6 26.1 %all_gather.18 = f32[2,2048]{1,0:T(2,128)S(1)} all-gather(f32[2,256]{1,0:T(2,128)S(1)} %multiply_subtract_fusion.1), channel_id=1, replica_groups=mesh['row'=4,'col'=8] {'col'}, dimensions={1}, use_global_device_ids=true | all-gather | bytes 18432 | tf_op jit(solution)/shard_map/all_gather | solution.py:93
  217.7 28.2 %while.49 = (s32[]{:T(128)}, f32[2,8,128]{2,1,0:T(8,128)S(1)}, s32[]{:T(128)}, s32[192]{0:T(256)S(1)}, f32[2,16,128]{2,0,1:T(2,128)S(1)}, /*index=5*/s32[]{:T(12...) while((s32[]{:T(128)}, f32[2,8,128]{2,1,0:T(8,128)S(1)}, ...), condition=%wide.region_19.21_spmd.clone.clone.clone, body=%wide.region_18.20_spmd.sunk.clone.clone.clone.sunk | while | flops 59296340 | bytes 1905783 | solution.py:103
  219.3 5.7 %fusion.269 = (pred[64]{0:T(512)(128)(4,1)S(1)}, s32[64]{0:T(128)S(1)}, pred[64]{0:T(512)(128)(4,1)S(1)}) fusion(s32[64]{0:T(128)S(1)} %gather_fusion.7, s32[]{:T(128)} %bitcast.234, s32[]{:T(128)} %bitcast.235, s32[]{:T(128)} %bitcast.236, s32[]{:T(128)} %bitcast.237, s32[]{:T(128)} %bitcast.238, s32[]{:T(128)} %bitcast.239, s32[]{:T(128)} %bitcast.240, ...), kind=kLoop, calls=%fused_computation.202.clone.1 | loop fusion | flops 2048 | bytes 1196 | tf_op jit(solution)/shard_map/while/body/eq | solution.py:87
  228.8 16.9 %fusion.272 = f32[2,64,128]{2,0,1:T(2,128)S(1)} fusion(f32[64,128]{1,0:T(8,128)S(1)} %bitcast.297, f32[64,128]{1,0:T(8,128)S(1)} %bitcast.306, f32[64,128]{1,0:T(8,128)S(1)} %bitcast.304, f32[64,128]{1,0:T(8,128)S(1)} %broadcast_add_fusion.21, f32[64,128]{1,0:T(8,128)S(1)} %bitcast.305, f32[64,128]{1,0:T(8,128)S(1)} %broadcast_add_fusion.22, ...), kind=kOutput, calls=%fused_computation.164.clone.1 | convolution fusion | flops 57671680 | bytes 409728 | tf_op jit(solution)/shard_map/while/body/gij,kgj->kgi/dot_general | solution.py:97
  245.9 1.0 copy.40
  247.0 42.1 %reduce-scatter.12.cloned.1.call-done = f32[256,2]{1,0:T(8,128)} async-done(((f32[1024,2]{1,0:T(8,128)}), f32[256,2]{1,0:T(8,128)}) %reduce-scatter.12.cloned.1.call-update) | async-done | bytes 2064
  290.3 39.3 %all-reduce.3 = (f32[2]{0:T(128)S(1)}, f32[2]{0:T(128)S(1)}) all-reduce(f32[2]{0:T(128)S(1)} %get-tuple-element.1152, f32[2]{0:T(128)S(1)} %get-tuple-element.1151), channel_id=1, replica_groups=mesh['row'=4,'col'=8] {'row','col'}, use_global_device_ids=true, to_apply=%region_17.19 | all-reduce | flops 4 | bytes 32 | tf_op jit(solution)/shard_map/psum | solution.py:42
  329.7 26.1 %all_gather.19 = f32[2,2048]{1,0:T(2,128)S(1)} all-gather(f32[2,256]{1,0:T(2,128)S(1)} %multiply_subtract_fusion), channel_id=1, replica_groups=mesh['row'=4,'col'=8] {'col'}, dimensions={1}, use_global_device_ids=true | all-gather | bytes 18432 | tf_op jit(solution)/shard_map/all_gather | solution.py:93
  355.8 28.2 %while.50 = (s32[]{:T(128)}, f32[2,8,128]{2,1,0:T(8,128)S(1)}, s32[]{:T(128)}, s32[192]{0:T(256)S(1)}, f32[2,16,128]{2,0,1:T(2,128)S(1)}, /*index=5*/s32[]{:T(12...) while((s32[]{:T(128)}, f32[2,8,128]{2,1,0:T(8,128)S(1)}, ...), condition=%wide.region_26.28_spmd.clone.clone.clone, body=%wide.region_25.27_spmd.sunk.clone.clone.clone.sunk | while | flops 59296340 | bytes 1905783 | solution.py:103
  357.4 5.7 %fusion.280 = (pred[64]{0:T(512)(128)(4,1)S(1)}, s32[64]{0:T(128)S(1)}, pred[64]{0:T(512)(128)(4,1)S(1)}) fusion(s32[64]{0:T(128)S(1)} %gather_fusion.13, s32[]{:T(128)} %bitcast.257, s32[]{:T(128)} %bitcast.258, s32[]{:T(128)} %bitcast.259, s32[]{:T(128)} %bitcast.260, s32[]{:T(128)} %bitcast.261, s32[]{:T(128)} %bitcast.262, s32[]{:T(128)} %bitcast.263, ...), kind=kLoop, calls=%fused_computation.295.clone.1 | loop fusion | flops 2048 | bytes 1196 | tf_op jit(solution)/shard_map/while/body/eq | solution.py:87
  366.9 16.9 %fusion.283 = f32[2,64,128]{2,0,1:T(2,128)S(1)} fusion(f32[64,128]{1,0:T(8,128)S(1)} %bitcast.298, f32[64,128]{1,0:T(8,128)S(1)} %bitcast.310, f32[64,128]{1,0:T(8,128)S(1)} %bitcast.308, f32[64,128]{1,0:T(8,128)S(1)} %broadcast_add_fusion.24, f32[64,128]{1,0:T(8,128)S(1)} %bitcast.309, f32[64,128]{1,0:T(8,128)S(1)} %broadcast_add_fusion.25, ...), kind=kOutput, calls=%fused_computation.257.clone.1 | convolution fusion | flops 57671680 | bytes 409728 | tf_op jit(solution)/shard_map/while/body/gij,kgj->kgi/dot_general | solution.py:97
  385.1 42.1 %reduce-scatter.14.cloned.1.call-done = f32[256,2]{1,0:T(8,128)} async-done(((f32[1024,2]{1,0:T(8,128)}), f32[256,2]{1,0:T(8,128)}) %reduce-scatter.14.cloned.1.call-update) | async-done | bytes 2064
  428.3 39.3 %all-reduce.2 = (f32[2]{0:T(128)S(1)}, f32[2]{0:T(128)S(1)}) all-reduce(f32[2]{0:T(128)S(1)} %get-tuple-element.1150, f32[2]{0:T(128)S(1)} %get-tuple-element.1149), channel_id=1, replica_groups=mesh['row'=4,'col'=8] {'row','col'}, use_global_device_ids=true, to_apply=%region_24.26 | all-reduce | flops 4 | bytes 32 | tf_op jit(solution)/shard_map/psum | solution.py:42
  467.8 41.0 %psum.55 = f32[2]{0:T(128)S(1)} all-reduce(f32[2]{0:T(128)S(1)} %get-tuple-element.1248), channel_id=1, replica_groups=mesh['row'=4,'col'=8] {'row','col'}, use_global_device_ids=true, to_apply=%region_31.33 | all-reduce | flops 2 | bytes 16 | tf_op jit(solution)/shard_map/psum | solution.py:128
  (118 shorter events, 29.2 us)
Async XLA Ops:
  6.5 144.5 %reduce-scatter.10.cloned.1.call-start = ((), (), s32[]{:S(2)}) async-start(), calls=%async_computation.3 | async-start | bytes 655360
  108.4 180.7 %reduce-scatter.12.cloned.1.call-start = ((), (), s32[]{:S(2)}) async-start(), calls=%async_computation.4 | async-start | bytes 655360
  247.0 180.2 %reduce-scatter.14.cloned.1.call-start = ((), (), s32[]{:S(2)}) async-start(), calls=%async_computation.5 | async-start | bytes 655360
Sparse Core Ops, SparseCore 0:
  108.6 42.4 reduce-scatter.9
  247.1 41.9 reduce-scatter.11
  385.2 41.9 reduce-scatter.13
where the time goes:
time: 519 us; the launch traced here: 518 us
  blocking collectives  275 us (53%)
  waiting for transfers between devices  127 us (24%)
  matrix products  51.2 us (10%)
  other arithmetic  25.5 us (5%)
  local copies, waits for them, and re-layouts  24 us (5%)
  between operations  15.2 us (3%)
    unnamed x6, waiting for transfers between devices  127 us
    psum x3, blocking collectives, paired_sums(): lax.psum((jnp.sum(residual * residual, axis=1), jnp.sum(residual * image,...  118 us
    all_gather x3, blocking collectives, apply(): lax.all_gather(direction, 'col', axis=1, tiled=True)  78.3 us
    dot_general x3, matrix products, turn(): jnp.einsum('gij,kgj->kgi', kern, remote[:, src_blk], precision=lax.Precis...  50.8 us
    psum x1, blocking collectives, per_device(): totals = lax.psum(jnp.sum(solution, axis=1), ('row', 'col'))  41 us
    all_gather x1, blocking collectives, per_device(): lax.all_gather(geo, 'col', axis=1, tiled=True).reshape(4, n_src, BLOCK)  32.4 us
    eq x3, other arithmetic, block_kernel(): tgt_ids[tgt_blk] == src_ids[src_blk]  17 us
  transfers between devices with their start and end apart: 3, of which 3 were waited for; matrix products, arithmetic and copies ran while one was open for 0% of the time, Pallas kernels for 0%

commit v1 on v0

--- a/solution.py
+++ b/solution.py
@@ -125,7 +125,7 @@
             direction = residual + ratio[:, None] * direction
             along = image + ratio[:, None] * along
             norm_now = norm_next
-    totals = lax.psum(jnp.sum(solution, axis=1), ("row", "col"))
+    totals = lax.psum(lax.psum(jnp.sum(solution, axis=1), "col"), "row")
     return solution[0] - totals[0] / totals[1] * solution[1]
 
 

time: 519 us -> 505 us (0.973)
  blocking collectives: 275 us -> 261 us
    psum x1 -> x2, blocking collectives: 41 us -> 26.7 us  [per_device(): totals = lax.psum(lax.psum(jnp.sum(solution, axis=1), 'col'), 'row')]
where the time goes in v1:
time: 505 us; the launch traced here: 504 us
  blocking collectives  261 us (52%)
  waiting for transfers between devices  127 us (25%)
  matrix products  51.2 us (10%)
  other arithmetic  25.5 us (5%)
  local copies, waits for them, and re-layouts  24 us (5%)
  between operations  15.2 us (3%)
    unnamed x6, waiting for transfers between devices  127 us
    psum x3, blocking collectives, paired_sums(): lax.psum((jnp.sum(residual * residual, axis=1), jnp.sum(residual * image,...  118 us
    all_gather x3, blocking collectives, apply(): lax.all_gather(direction, 'col', axis=1, tiled=True)  78.3 us
    dot_general x3, matrix products, turn(): jnp.einsum('gij,kgj->kgi', kern, remote[:, src_blk], precision=lax.Precis...  50.8 us
    all_gather x1, blocking collectives, per_device(): lax.all_gather(geo, 'col', axis=1, tiled=True).reshape(4, n_src, BLOCK)  32.4 us
    psum x2, blocking collectives, per_device(): totals = lax.psum(lax.psum(jnp.sum(solution, axis=1), 'col'), 'row')  26.7 us
    eq x3, other arithmetic, block_kernel(): tgt_ids[tgt_blk] == src_ids[src_blk]  17 us
  transfers between devices with their start and end apart: 3, of which 3 were waited for; matrix products, arithmetic and copies ran while one was open for 0% of the time, Pallas kernels for 0%

profile of v1, /device:TPU:0, one launch (start us, length us, event | category | flops | bytes accessed | tf_op | source)
XLA Modules:
  0.0 503.6 jit_solution(10917904094071344808)
XLA Ops:
  6.5 1.4 fusion.200
  10.3 32.4 %all_gather.16 = f32[4,2048]{1,0:T(4,128)S(1)} all-gather(f32[4,256]{1,0:T(4,128)S(1)} %pad_maximum_fusion), channel_id=1, replica_groups=mesh['row'=4,'col'=8] {'col'}, dimensions={1}, use_global_device_ids=true | all-gather | bytes 36864 | tf_op jit(solution)/shard_map/all_gather | solution.py:62
  42.7 5.2 %all_gather.17 = f32[4,1024]{1,0:T(4,128)S(1)} all-gather(f32[4,256]{1,0:T(4,128)S(1)} %pad_maximum_fusion), channel_id=1, replica_groups=mesh['row'=4,'col'=8] {'row'}, dimensions={1}, use_global_device_ids=true | all-gather | bytes 20480 | tf_op jit(solution)/shard_map/all_gather | solution.py:63
  49.1 1.4 scatter_custom_fusion
  52.3 26.1 %all_gather.15 = f32[2,2048]{1,0:T(2,128)S(1)} all-gather(f32[2,256]{1,0:T(2,128)S(1)} %stack.2), channel_id=1, replica_groups=mesh['row'=4,'col'=8] {'col'}, dimensions={1}, use_global_device_ids=true | all-gather | bytes 18432 | tf_op jit(solution)/shard_map/all_gather | solution.py:93
  79.2 28.1 %while.48 = (s32[]{:T(128)}, f32[2,8,128]{2,1,0:T(8,128)S(1)}, s32[]{:T(128)}, s32[192]{0:T(256)S(1)}, f32[2,16,128]{2,0,1:T(2,128)S(1)}, /*index=5*/s32[]{:T(12...) while((s32[]{:T(128)}, f32[2,8,128]{2,1,0:T(8,128)S(1)}, ...), condition=%wide.region_11.13_spmd.clone.clone.clone, body=%wide.region_10.12_spmd.sunk.clone.clone.clone.sunk | while | flops 59296340 | bytes 1905783 | solution.py:103
  80.8 5.6 %fusion.258 = (pred[64]{0:T(512)(128)(4,1)S(1)}, s32[64]{0:T(128)S(1)}, pred[64]{0:T(512)(128)(4,1)S(1)}) fusion(s32[64]{0:T(128)S(1)} %gather_fusion.1, s32[]{:T(128)} %bitcast.211, s32[]{:T(128)} %bitcast.212, s32[]{:T(128)} %bitcast.213, s32[]{:T(128)} %bitcast.214, s32[]{:T(128)} %bitcast.215, s32[]{:T(128)} %bitcast.216, s32[]{:T(128)} %bitcast.217, ...), kind=kLoop, calls=%fused_computation.109.clone.1 | loop fusion | flops 2048 | bytes 1196 | tf_op jit(solution)/shard_map/while/body/eq | solution.py:87
  90.3 16.9 %fusion.261 = f32[2,64,128]{2,0,1:T(2,128)S(1)} fusion(f32[64,128]{1,0:T(8,128)S(1)} %bitcast.296, f32[64,128]{1,0:T(8,128)S(1)} %bitcast.302, f32[64,128]{1,0:T(8,128)S(1)} %bitcast.300, f32[64,128]{1,0:T(8,128)S(1)} %broadcast_add_fusion.18, f32[64,128]{1,0:T(8,128)S(1)} %bitcast.301, f32[64,128]{1,0:T(8,128)S(1)} %broadcast_add_fusion.19, ...), kind=kOutput, calls=%fused_computation.71.clone.1 | convolution fusion | flops 57671680 | bytes 409728 | tf_op jit(solution)/shard_map/while/body/gij,kgj->kgi/dot_general | solution.py:97
  108.5 42.6 %reduce-scatter.10.cloned.1.call-done = f32[256,2]{1,0:T(8,128)} async-done(((f32[1024,2]{1,0:T(8,128)}), f32[256,2]{1,0:T(8,128)}) %reduce-scatter.10.cloned.1.call-update) | async-done | bytes 2064
  152.2 39.3 %all-reduce.4 = (f32[2]{0:T(128)S(1)}, f32[2]{0:T(128)S(1)}) all-reduce(f32[2]{0:T(128)S(1)} %get-tuple-element.1154, f32[2]{0:T(128)S(1)} %get-tuple-element.1153), channel_id=1, replica_groups=mesh['row'=4,'col'=8] {'row','col'}, use_global_device_ids=true, to_apply=%region_2.3 | all-reduce | flops 4 | bytes 32 | tf_op jit(solution)/shard_map/psum | solution.py:42
  191.6 26.1 %all_gather.18 = f32[2,2048]{1,0:T(2,128)S(1)} all-gather(f32[2,256]{1,0:T(2,128)S(1)} %multiply_subtract_fusion.1), channel_id=1, replica_groups=mesh['row'=4,'col'=8] {'col'}, dimensions={1}, use_global_device_ids=true | all-gather | bytes 18432 | tf_op jit(solution)/shard_map/all_gather | solution.py:93
  217.7 28.2 %while.49 = (s32[]{:T(128)}, f32[2,8,128]{2,1,0:T(8,128)S(1)}, s32[]{:T(128)}, s32[192]{0:T(256)S(1)}, f32[2,16,128]{2,0,1:T(2,128)S(1)}, /*index=5*/s32[]{:T(12...) while((s32[]{:T(128)}, f32[2,8,128]{2,1,0:T(8,128)S(1)}, ...), condition=%wide.region_19.21_spmd.clone.clone.clone, body=%wide.region_18.20_spmd.sunk.clone.clone.clone.sunk | while | flops 59296340 | bytes 1905783 | solution.py:103
  219.3 5.7 %fusion.269 = (pred[64]{0:T(512)(128)(4,1)S(1)}, s32[64]{0:T(128)S(1)}, pred[64]{0:T(512)(128)(4,1)S(1)}) fusion(s32[64]{0:T(128)S(1)} %gather_fusion.7, s32[]{:T(128)} %bitcast.234, s32[]{:T(128)} %bitcast.235, s32[]{:T(128)} %bitcast.236, s32[]{:T(128)} %bitcast.237, s32[]{:T(128)} %bitcast.238, s32[]{:T(128)} %bitcast.239, s32[]{:T(128)} %bitcast.240, ...), kind=kLoop, calls=%fused_computation.202.clone.1 | loop fusion | flops 2048 | bytes 1196 | tf_op jit(solution)/shard_map/while/body/eq | solution.py:87
  228.8 16.9 %fusion.272 = f32[2,64,128]{2,0,1:T(2,128)S(1)} fusion(f32[64,128]{1,0:T(8,128)S(1)} %bitcast.297, f32[64,128]{1,0:T(8,128)S(1)} %bitcast.306, f32[64,128]{1,0:T(8,128)S(1)} %bitcast.304, f32[64,128]{1,0:T(8,128)S(1)} %broadcast_add_fusion.21, f32[64,128]{1,0:T(8,128)S(1)} %bitcast.305, f32[64,128]{1,0:T(8,128)S(1)} %broadcast_add_fusion.22, ...), kind=kOutput, calls=%fused_computation.164.clone.1 | convolution fusion | flops 57671680 | bytes 409728 | tf_op jit(solution)/shard_map/while/body/gij,kgj->kgi/dot_general | solution.py:97
  247.0 42.1 %reduce-scatter.12.cloned.1.call-done = f32[256,2]{1,0:T(8,128)} async-done(((f32[1024,2]{1,0:T(8,128)}), f32[256,2]{1,0:T(8,128)}) %reduce-scatter.12.cloned.1.call-update) | async-done | bytes 2064
  290.3 39.3 %all-reduce.3 = (f32[2]{0:T(128)S(1)}, f32[2]{0:T(128)S(1)}) all-reduce(f32[2]{0:T(128)S(1)} %get-tuple-element.1152, f32[2]{0:T(128)S(1)} %get-tuple-element.1151), channel_id=1, replica_groups=mesh['row'=4,'col'=8] {'row','col'}, use_global_device_ids=true, to_apply=%region_17.19 | all-reduce | flops 4 | bytes 32 | tf_op jit(solution)/shard_map/psum | solution.py:42
  329.7 26.1 %all_gather.19 = f32[2,2048]{1,0:T(2,128)S(1)} all-gather(f32[2,256]{1,0:T(2,128)S(1)} %multiply_subtract_fusion), channel_id=1, replica_groups=mesh['row'=4,'col'=8] {'col'}, dimensions={1}, use_global_device_ids=true | all-gather | bytes 18432 | tf_op jit(solution)/shard_map/all_gather | solution.py:93
  355.8 28.2 %while.50 = (s32[]{:T(128)}, f32[2,8,128]{2,1,0:T(8,128)S(1)}, s32[]{:T(128)}, s32[192]{0:T(256)S(1)}, f32[2,16,128]{2,0,1:T(2,128)S(1)}, /*index=5*/s32[]{:T(12...) while((s32[]{:T(128)}, f32[2,8,128]{2,1,0:T(8,128)S(1)}, ...), condition=%wide.region_26.28_spmd.clone.clone.clone, body=%wide.region_25.27_spmd.sunk.clone.clone.clone.sunk | while | flops 59296340 | bytes 1905783 | solution.py:103
  357.4 5.7 %fusion.280 = (pred[64]{0:T(512)(128)(4,1)S(1)}, s32[64]{0:T(128)S(1)}, pred[64]{0:T(512)(128)(4,1)S(1)}) fusion(s32[64]{0:T(128)S(1)} %gather_fusion.13, s32[]{:T(128)} %bitcast.257, s32[]{:T(128)} %bitcast.258, s32[]{:T(128)} %bitcast.259, s32[]{:T(128)} %bitcast.260, s32[]{:T(128)} %bitcast.261, s32[]{:T(128)} %bitcast.262, s32[]{:T(128)} %bitcast.263, ...), kind=kLoop, calls=%fused_computation.295.clone.1 | loop fusion | flops 2048 | bytes 1196 | tf_op jit(solution)/shard_map/while/body/eq | solution.py:87
  366.9 16.9 %fusion.283 = f32[2,64,128]{2,0,1:T(2,128)S(1)} fusion(f32[64,128]{1,0:T(8,128)S(1)} %bitcast.298, f32[64,128]{1,0:T(8,128)S(1)} %bitcast.310, f32[64,128]{1,0:T(8,128)S(1)} %bitcast.308, f32[64,128]{1,0:T(8,128)S(1)} %broadcast_add_fusion.24, f32[64,128]{1,0:T(8,128)S(1)} %bitcast.309, f32[64,128]{1,0:T(8,128)S(1)} %broadcast_add_fusion.25, ...), kind=kOutput, calls=%fused_computation.257.clone.1 | convolution fusion | flops 57671680 | bytes 409728 | tf_op jit(solution)/shard_map/while/body/gij,kgj->kgi/dot_general | solution.py:97
  385.1 42.1 %reduce-scatter.14.cloned.1.call-done = f32[256,2]{1,0:T(8,128)} async-done(((f32[1024,2]{1,0:T(8,128)}), f32[256,2]{1,0:T(8,128)}) %reduce-scatter.14.cloned.1.call-update) | async-done | bytes 2064
  428.3 39.3 %all-reduce.2 = (f32[2]{0:T(128)S(1)}, f32[2]{0:T(128)S(1)}) all-reduce(f32[2]{0:T(128)S(1)} %get-tuple-element.1150, f32[2]{0:T(128)S(1)} %get-tuple-element.1149), channel_id=1, replica_groups=mesh['row'=4,'col'=8] {'row','col'}, use_global_device_ids=true, to_apply=%region_24.26 | all-reduce | flops 4 | bytes 32 | tf_op jit(solution)/shard_map/psum | solution.py:42
  467.8 21.1 %psum.62 = f32[2]{0:T(128)S(1)} all-reduce(f32[2]{0:T(128)S(1)} %get-tuple-element.1248), channel_id=1, replica_groups=mesh['row'=4,'col'=8] {'col'}, use_global_device_ids=true, to_apply=%region_31.33 | all-reduce | flops 2 | bytes 16 | tf_op jit(solution)/shard_map/psum | solution.py:128
  488.9 5.6 %psum.63 = f32[2]{0:T(128)S(1)} all-reduce(f32[2]{0:T(128)S(1)} %psum.62), channel_id=1, replica_groups=mesh['row'=4,'col'=8] {'row'}, use_global_device_ids=true, to_apply=%region_32.34 | all-reduce | flops 2 | bytes 16 | tf_op jit(solution)/shard_map/psum | solution.py:128
  (119 shorter events, 30.2 us)
Async XLA Ops:
  6.5 144.5 %reduce-scatter.10.cloned.1.call-start = ((), (), s32[]{:S(2)}) async-start(), calls=%async_computation.3 | async-start | bytes 655360
  108.4 180.7 %reduce-scatter.12.cloned.1.call-start = ((), (), s32[]{:S(2)}) async-start(), calls=%async_computation.4 | async-start | bytes 655360
  247.0 180.2 %reduce-scatter.14.cloned.1.call-start = ((), (), s32[]{:S(2)}) async-start(), calls=%async_computation.5 | async-start | bytes 655360
Sparse Core Ops, SparseCore 0:
  108.6 42.4 reduce-scatter.9
  247.1 41.9 reduce-scatter.11
  385.2 41.9 reduce-scatter.13
